TPU v7x, 128 devices: a whole 4x4x4 slice. The times are simulated.
128 devices in a mesh: dp: 64 (over z, y, x), tensor: 2 (over core).
Axes of the slice: x: 4, y: 4, z: 4, core: 2. Of those that a mesh axis runs over, the one named last changes fastest.
Arguments:
- encoded: bfloat16 [131072, 1152], P('dp', 'tensor'), may hold values from -9 to 9
- counts: int32 [2048], P('dp'), may hold values from 16 to 64
- win_ids: int32 [2048, 64], P('dp'), may hold values from 0 to 31, never falling along the last dimension, each value on 1 to 8 neighbouring positions
- dest_seq: int32 [2048], P('dp'), may hold values from 0 to 63, as said below
- dest_slot: int32 [2048], P('dp'), may hold values from 0 to 31, as said below
- w_first: bfloat16 [1152, 4608], P(None, 'tensor'), may hold values from -0.3125 to 0.3125
- b_first: float32 [4608], P('tensor'), may hold values from -3 to 3
- w_second: bfloat16 [4608, 2304], P('tensor'), may hold values from -0.1875 to 0.1875
- b_second: float32 [2304], P('tensor'), may hold values from -3 to 3
Outputs:
- projected: bfloat16 [65536, 2304], P('dp', 'tensor')
Inputs may be any that keep to these rules, and one draw needn't show every extreme that they name: `dest_seq`: every sequence receives exactly 32 samples, no two of them from the same index of dp. `dest_slot`: the samples that one sequence receives have distinct block offsets.
All inputs are finite; a program needn't handle non-finite values.
Results may differ from a plain program's by a relative error of at most 0.009.
Values may be sent and summed in bfloat16 or wider, within the bound.
A program may use at most 128 MiB of HBM per device.

v0:
```python
import jax
import jax.numpy as jnp
from jax import lax
from jax.sharding import PartitionSpec as P

BLOCK = 32


def from_everyone(array, axis):
    copies = jnp.broadcast_to(array, (lax.axis_size(axis), *array.shape))
    return lax.all_to_all(copies, axis, split_axis=0, concat_axis=0, tiled=True)


def laid_out(parts, dim):
    lengths = list(parts.shape[1:])
    lengths[dim] *= parts.shape[0]
    return jnp.moveaxis(parts, 0, dim).reshape(lengths)


def gathered_copies(array, axis, dim):
    parts = from_everyone(array, axis)
    return laid_out(parts, dim)


def cut_along(array, dim, count):
    lengths = array.shape
    parts = array.reshape(*lengths[:dim], count, lengths[dim] // count, *lengths[dim + 1 :])
    return jnp.moveaxis(parts, dim, 0)


def sum_at_owner(array, axis, dim):
    parts = cut_along(array, dim, lax.axis_size(axis))
    arrived = lax.all_to_all(parts, axis, split_axis=0, concat_axis=0, tiled=True)
    return arrived.astype(jnp.float32).sum(axis=0)


def pool_blocks(ids_live, tokens):
    windows = jnp.arange(BLOCK, dtype=jnp.int32)
    onehot = ids_live[:, None, :] == windows[None, :, None]
    number = jnp.sum(onehot.astype(jnp.float32), axis=2)
    totals = jnp.einsum(
        "nwc,ncf->nwf", onehot.astype(jnp.bfloat16), tokens, preferred_element_type=jnp.float32
    )
    return (totals / jnp.maximum(number, 1.0)[:, :, None]).astype(jnp.bfloat16)


def shards(encoded, counts, win_ids, dest_seq, dest_slot, w_first, b_first, w_second, b_second):
    samples = counts.shape[0]
    capacity = win_ids.shape[1]
    tokens = encoded.reshape(samples, capacity, encoded.shape[1])
    positions = jnp.arange(capacity, dtype=jnp.int32)
    ids_live = jnp.where(positions[None, :] < counts[:, None], win_ids, -1)
    groups = lax.axis_size("dp")
    targets = jnp.arange(groups, dtype=jnp.int32)
    chosen = dest_seq[None, :] == targets[:, None]
    picker = chosen.astype(jnp.bfloat16)
    offset_plus = jnp.sum(jnp.where(chosen, dest_slot[None, :] + 1, 0), axis=1)[:, None]
    pooled = pool_blocks(ids_live, tokens)
    outgoing = jnp.einsum("es,swf->ewf", picker, pooled, preferred_element_type=jnp.float32).astype(
        jnp.bfloat16
    )
    arrived, got_offset = (
        lax.all_to_all(outgoing, "dp", split_axis=0, concat_axis=0, tiled=True),
        lax.all_to_all(
            offset_plus.astype(jnp.bfloat16), "dp", split_axis=0, concat_axis=0, tiled=True
        ),
    )
    got_offset = got_offset.astype(jnp.int32)
    slot_from = got_offset[:, 0] - 1
    slot_ids = jnp.arange(samples, dtype=jnp.int32)
    placer = (slot_from[None, :] == slot_ids[:, None]).astype(jnp.bfloat16)
    packed = jnp.einsum("kd,dwf->kwf", placer, arrived, preferred_element_type=jnp.float32).astype(
        jnp.bfloat16
    )
    packed = packed.reshape(samples * arrived.shape[1], arrived.shape[2])
    preact = (
        jnp.dot(gathered_copies(packed, "tensor", 1), w_first, preferred_element_type=jnp.float32)
        + b_first
    )
    hidden = jax.nn.gelu(preact, approximate=True).astype(jnp.bfloat16)
    partial_value = jnp.dot(hidden, w_second, preferred_element_type=jnp.float32)
    summed = sum_at_owner(partial_value.astype(jnp.bfloat16), "tensor", 1)
    return (summed + b_second).astype(jnp.bfloat16)


def solution(mesh):
    placed = (
        P("dp", "tensor"),
        P("dp"),
        P("dp", None),
        P("dp"),
        P("dp"),
        P(None, "tensor"),
        P("tensor"),
        P("tensor", None),
        P("tensor"),
    )
    return jax.shard_map(
        shards, mesh=mesh, in_specs=placed, out_specs=P("dp", "tensor"), check_vma=False
    )
```

profile of v0, /device:TPU:1, one launch (start us, length us, event | category | flops | bytes accessed | tf_op | source)
XLA Modules:
  0.0 117.1 jit_solution(11122180019414638289)
XLA Ops:
  0.0 0.7 broadcast_add_fusion
  0.7 0.7 select_reduce_fusion
  1.4 0.7 copy.21
  2.1 12.0 %all-to-all-start = ((bf16[64,1,1]{2,1,0:T(2,128)(2,1)}), bf16[64,1,1]{2,1,0:T(2,128)(2,1)S(1)}, u32[]{:S(2)}, u32[]{:S(2)}) async-start(bf16[64,1,1]{2,1,0:T(2,128)(2,1)} %copy.21), calls=%async_computation | async-start | bytes 65536 | tf_op jit(solution)/shard_map/all_to_all | solution.py:64
  14.1 0.8 fusion.26
  14.9 0.2 convert_reduce_fusion.1
  15.1 3.1 %copy.22 = bf16[2048,576]{1,0:T(8,128)(2,1)S(1)} copy(bf16[2048,576]{0,1:T(8,128)(2,1)} %param.9) | data formatting | bytes 4718592 | tf_op args[0]
  18.2 0.6 divide_convert_fusion
  18.8 0.1 copy-done.1
  18.9 1.0 convolution_convert_fusion
  19.8 3.0 %copy.24 = bf16[64,32,576]{2,1,0:T(8,128)(2,1)} copy(bf16[64,32,576]{2,0,1:T(8,128)(2,1)S(1)} %convolution_convert_fusion) | data formatting | bytes 4718592 | tf_op jit(solution)/shard_map/convert_element_type | solution.py:59
  22.9 9.8 %all-to-all-start.1 = ((bf16[64,32,576]{2,1,0:T(8,128)(2,1)}), bf16[64,32,576]{2,1,0:T(8,128)(2,1)S(1)}, u32[]{:S(2)}, u32[]{:S(2)}) async-start(bf16[64,32,576]{2,1,0:T(8,128)(2,1)} %copy.24), calls=%async_computation.1 | async-start | bytes 5242880 | tf_op jit(solution)/shard_map/all_to_all | solution.py:63
  32.6 1.2 %add_reduce_fusion = s32[64]{0:T(128)S(1)} fusion(bf16[64,1,1]{2,1,0:T(2,128)(2,1)S(1)} %all-to-all-done), kind=kLoop, calls=%fused_computation.28 | loop fusion | flops 128 | bytes 384 | tf_op jit(solution)/shard_map/sub | solution.py:69
  33.9 32.3 %all-to-all-done.1 = bf16[64,32,576]{2,1,0:T(8,128)(2,1)S(1)} async-done(((bf16[64,32,576]{2,1,0:T(8,128)(2,1)}), bf16[64,32,576]{2,1,0:T(8,128)(2,1)S(1)}, u32[]{:S(2)}, u32[]{:S(2)}) %all-to-all-start.1) | async-done | bytes 2359328 | tf_op jit(solution)/shard_map/all_to_all | solution.py:63
  66.2 1.2 fusion.17
  67.4 0.4 copy.26
  67.8 0.6 copy.27
  68.5 0.3 broadcast_in_dim.21
  68.7 8.1 %all_to_all.21 = bf16[2,1024,576]{1,2,0:T(8,128)(2,1)S(1)} all-to-all(bf16[2,1024,576]{1,2,0:T(8,128)(2,1)S(1)} %broadcast_in_dim.21), channel_id=1, replica_groups=mesh['dp'=64,'tensor'=2] {'tensor'}, dimensions={0} | all-to-all | bytes 4718592 | tf_op jit(solution)/shard_map/all_to_all | solution.py:11
  76.9 27.4 %fusion.9 = bf16[1024,2304]{1,0:T(8,128)(2,1)} fusion(bf16[2304,2304]{1,0:T(8,128)(2,1)} %param.16, bf16[1024,1152]{0,1:T(8,128)(2,1)S(1)} %bitcast.28, bf16[1152,2304]{1,0:T(8,128)(2,1)} %param.14, f32[2304]{0:T(1024)S(1)} %copy-done.2), kind=kOutput, calls=%fused_computation.11 | convolution fusion | flops 16333406208 | bytes 23012352 | tf_op jit(solution)/shard_map/dot_general | solution.py:81
  104.3 2.7 %copy.37 = bf16[128,2,8,1152]{3,2,0,1:T(8,128)(2,1)S(1)} copy(bf16[128,2,8,1152]{3,2,1,0:T(8,128)(2,1)} %bitcast.26) | data formatting | bytes 9437184 | tf_op jit(solution)/shard_map/reshape | solution.py:27
  107.0 7.5 %all_to_all.22 = bf16[2,1024,1152]{2,1,0:T(8,128)(2,1)S(1)} all-to-all(bf16[2,1024,1152]{2,1,0:T(8,128)(2,1)S(1)} %bitcast.24), channel_id=1, replica_groups=mesh['dp'=64,'tensor'=2] {'tensor'}, dimensions={0} | all-to-all | bytes 9437184 | tf_op jit(solution)/shard_map/all_to_all | solution.py:33
  114.5 0.8 convert_reduce_fusion
  115.4 1.8 %add_convert_fusion = bf16[1024,1152]{1,0:T(8,128)(2,1)} fusion(f32[1024,1152]{1,0:T(8,128)S(1)} %convert_reduce_fusion, f32[1152]{0:T(1024)S(1)} %copy-done), kind=kLoop, calls=%fused_computation.13 | loop fusion | flops 2359296 | bytes 7082496 | tf_op jit(solution)/shard_map/convert_element_type | solution.py:83
  (8 shorter events, 0.0 us)
Async XLA Ops:
  2.1 20.7 %all-to-all-start = ((bf16[64,1,1]{2,1,0:T(2,128)(2,1)}), bf16[64,1,1]{2,1,0:T(2,128)(2,1)S(1)}, u32[]{:S(2)}, u32[]{:S(2)}) async-start(bf16[64,1,1]{2,1,0:T(2,128)(2,1)} %copy.21), calls=%async_computation | async-start | bytes 65536 | tf_op jit(solution)/shard_map/all_to_all | solution.py:64
  18.2 0.7 copy-start.1
  22.9 43.4 %all-to-all-start.1 = ((bf16[64,32,576]{2,1,0:T(8,128)(2,1)}), bf16[64,32,576]{2,1,0:T(8,128)(2,1)S(1)}, u32[]{:S(2)}, u32[]{:S(2)}) async-start(bf16[64,32,576]{2,1,0:T(8,128)(2,1)} %copy.24), calls=%async_computation.1 | async-start | bytes 5242880 | tf_op jit(solution)/shard_map/all_to_all | solution.py:63
  68.4 8.4 %copy-start.2 = (f32[2304]{0:T(1024)S(1)}, f32[2304]{0:T(1024)}, u32[]{:S(2)}) copy-start(f32[2304]{0:T(1024)} %param.15) | copy-start | bytes 27652
  114.5 0.9 copy-start
where the time goes:
time: 118 us; the launch traced here: 117 us
  waiting for transfers between devices  32.4 us (27%)
  matrix products  30.1 us (26%)
  starting transfers between devices  21.7 us (18%)
  blocking collectives  15.6 us (13%)
  local copies, waits for them, and re-layouts  10.9 us (9%)
  other arithmetic  6.25 us (5%)
    all_to_all x1, waiting for transfers between devices, shards(): lax.all_to_all(outgoing, 'dp', split_axis=0, concat_axis=0, tiled=True)  32.3 us
    dot_general x1, matrix products, shards(): jnp.dot(hidden, w_second, preferred_element_type=jnp.float32)  27.4 us
    all_to_all x1, starting transfers between devices, shards(): lax.all_to_all(offset_plus.astype(jnp.bfloat16), 'dp', split_axis=0, conc...  12 us
    all_to_all x1, starting transfers between devices, shards(): lax.all_to_all(outgoing, 'dp', split_axis=0, concat_axis=0, tiled=True)  9.77 us
    all_to_all x1, blocking collectives, from_everyone(): return lax.all_to_all(copies, axis, split_axis=0, concat_axis=0, tiled=True)  8.12 us
    all_to_all x1, blocking collectives, sum_at_owner(): lax.all_to_all(parts, axis, split_axis=0, concat_axis=0, tiled=True)  7.53 us
    unnamed x7, local copies, waits for them, and re-layouts  3.19 us
    convert_element_type x1, local copies, waits for them, and re-layouts, shards(): jnp.einsum('es,swf->ewf', picker, pooled, preferred_element_type=jnp.floa...  3.01 us
  transfers between devices with their start and end apart: 2, of which 1 were waited for; matrix products, arithmetic and copies ran while one was open for 8% of the time, Pallas kernels for 0%

commit v1 on v0

v1 whole, which is shorter than its diff:
```python
import functools

import jax
import jax.numpy as jnp
from jax import lax
from jax.experimental import pallas as pl
from jax.experimental.pallas import tpu as pltpu
from jax.sharding import PartitionSpec as P

MESH = pl.DeviceIdType.MESH
BF = jnp.bfloat16
F32 = jnp.float32
I32 = jnp.int32

GROUPS = 64
SAMP = 32
CAP = 64
BLOCK = 32
FH = 576
MAIN = 512
OUT = 1152
HID = 2304
CHUNKS = ((8, 0), (4, 16), (4, 24))
PAD = 640


def iota(shape, dim):
    return lax.broadcasted_iota(I32, shape, dim)


def target_of(me, step):
    off = lax.rem(step * 37, GROUPS)
    z = lax.rem(me // 16 + off // 16, 4)
    y = lax.rem(lax.rem(me // 4, 4) + lax.rem(off // 4, 4), 4)
    x = lax.rem(lax.rem(me, 4) + lax.rem(off, 4), 4)
    return z * 16 + y * 4 + x


def kernel(
    counts, dest_seq, dest_slot, win_ids, b_first, b_second, enc, w_first, w_second,
    out,
    tok, w1, w2, pooled0, pooled1, pooled2, snd0, snd1, snd2, arr0, arr1, arr2,
    meta_out, meta_in, xf0, xf1, xf2, hid, ps0, ps1, ps2, pr0, pr1, pr2, po,
    enc_sem, w_sem, meta_s, meta_r, a_s, a_r, x_s, x_r, p_s, p_r,
):
    me = lax.axis_index("dp")
    core = lax.axis_index("tensor")
    other = 1 - core
    pooled, snd, arr = (pooled0, pooled1, pooled2), (snd0, snd1, snd2), (arr0, arr1, arr2)
    xf, ps, pr = (xf0, xf1, xf2), (ps0, ps1, ps2), (pr0, pr1, pr2)

    barrier = pltpu.get_barrier_semaphore()

    def greet(step, _):
        pl.semaphore_signal(
            barrier, inc=1, device_id=(target_of(me, step), core), device_id_type=MESH
        )
        return 0

    lax.fori_loop(1, GROUPS, greet, 0)
    pl.semaphore_signal(barrier, inc=1, device_id=(me, other), device_id_type=MESH)

    enc_copy = pltpu.make_async_copy(enc, tok, enc_sem)
    enc_copy.start()

    w_copies = []
    for side, base in ((0, core * FH), (1, other * FH)):
        at = side * PAD
        w_copies += [(w_first.at[pl.ds(pl.multiple_of(base, 64), MAIN)], w1.at[pl.ds(at, MAIN)])]
        for twice in range(2):
            w_copies += [
                (
                    w_first.at[pl.ds(pl.multiple_of(base + MAIN, 64), 64)],
                    w1.at[pl.ds(at + MAIN + 64 * twice, 64)],
                )
            ]
    w_copies += [
        (w_second.at[:, pl.ds(pl.multiple_of(other * OUT, 128), OUT)], w2.at[:, pl.ds(0, OUT)]),
        (w_second.at[:, pl.ds(pl.multiple_of(core * OUT, 128), OUT)], w2.at[:, pl.ds(OUT, OUT)]),
    ]
    w_copies = [
        pltpu.make_async_copy(src, dst, w_sem.at[i]) for i, (src, dst) in enumerate(w_copies)
    ]

    row = iota((GROUPS, 128), 0)
    meta = jnp.zeros((GROUPS, 128), I32)
    for s in range(SAMP):
        meta = jnp.where(row == dest_seq[s], dest_slot[s] + 1, meta)
    meta_out[...] = meta.reshape(GROUPS, 1, 128)
    meta_in[pl.ds(me, 1)] = meta_out[pl.ds(me, 1)]

    ids = iota((SAMP, CAP), 1)
    srow = iota((SAMP, CAP), 0)
    limit = jnp.zeros((SAMP, CAP), I32)
    for s in range(SAMP):
        limit = jnp.where(srow == s, counts[s], limit)
    live = jnp.where(ids < limit, win_ids[...], -1)

    rho = iota((128, 256), 0)
    wmap = jnp.zeros((128, 256), I32)
    smap = jnp.zeros((128, 256), I32)
    base = 0
    for rows, first in CHUNKS:
        q = rho - base
        inside = (q >= 0) & (q < 8 * rows)
        h = q // (4 * rows)
        wmap = jnp.where(inside, first + h * rows + q % rows, wmap)
        smap = jnp.where(inside, (q // rows) % 4, smap)
        base += 8 * rows
    same = smap == iota((128, 256), 1) // CAP

    enc_copy.wait()
    for copy in w_copies:
        copy.start()

    for g in range(SAMP // 4):
        line = jnp.concatenate([live[4 * g + i : 4 * g + i + 1, :] for i in range(4)], axis=1)
        onehot = jnp.where((wmap == line) & same, 1.0, 0.0).astype(F32)
        number = jnp.sum(onehot, axis=1, keepdims=True)
        totals = lax.dot_general(
            onehot.astype(BF),
            tok[:, pl.ds(256 * g, 256)],
            (((1,), (1,)), ((), ())),
            preferred_element_type=F32,
        )
        mean = totals * (1.0 / jnp.maximum(number, 1.0))
        base = 0
        for c, (rows, _) in enumerate(CHUNKS):
            n = 4 * rows
            lo, hi = mean[base : base + n], mean[base + n : base + 2 * n]
            packed = jnp.concatenate(
                [lo[:, :MAIN], hi[:, :MAIN], lo[:, MAIN:], hi[:, MAIN:]], axis=1
            )
            pooled[c][pl.ds(n * g, n), :] = packed.astype(BF)
            base += 2 * n

    pl.semaphore_wait(barrier, GROUPS)

    def send_meta(step, _):
        to = target_of(me, step)
        pltpu.make_async_remote_copy(
            src_ref=meta_out.at[pl.ds(to, 1)],
            dst_ref=meta_in.at[pl.ds(me, 1)],
            send_sem=meta_s,
            recv_sem=meta_r,
            device_id=(to, core),
            device_id_type=MESH,
        ).start()
        return 0

    for c, (rows, _) in enumerate(CHUNKS):
        lanes = SAMP * rows
        where = jnp.zeros((8, lanes), I32)
        lane_s = iota((8, lanes), 1) // rows
        for s in range(SAMP):
            where = jnp.where(lane_s == s, dest_seq[s], where)
        shape = (GROUPS * rows, lanes)
        pick = (iota(shape, 0) // rows == where[0:1]) & (
            iota(shape, 0) % rows == iota(shape, 1) % rows
        )
        pick = jnp.where(pick, 1.0, 0.0).astype(BF)
        chosen = jnp.dot(pick, pooled[c][...], preferred_element_type=F32)
        snd[c][...] = chosen.reshape(GROUPS, rows, 2 * FH).astype(BF)
        arr[c][pl.ds(me, 1)] = snd[c][pl.ds(me, 1)]

        def send(step, _, c=c):
            to = target_of(me, step)
            pltpu.make_async_remote_copy(
                src_ref=snd[c].at[pl.ds(to, 1)],
                dst_ref=arr[c].at[pl.ds(me, 1)],
                send_sem=a_s.at[c],
                recv_sem=a_r.at[c],
                device_id=(to, core),
                device_id_type=MESH,
            ).start()
            return 0

        if c == 0:
            lax.fori_loop(1, GROUPS, send_meta, 0)
        lax.fori_loop(1, GROUPS, send, 0)

    def whole(src, dst, send_sem, recv_sem):
        return pltpu.make_async_remote_copy(
            src_ref=src.at[pl.ds(0, GROUPS - 1)],
            dst_ref=dst.at[pl.ds(0, GROUPS - 1)],
            send_sem=send_sem,
            recv_sem=recv_sem,
            device_id=(me, other),
            device_id_type=MESH,
        )

    def to_partner(src, dst, send_sem, recv_sem):
        return pltpu.make_async_remote_copy(
            src_ref=src,
            dst_ref=dst,
            send_sem=send_sem,
            recv_sem=recv_sem,
            device_id=(me, other),
            device_id_type=MESH,
        )

    whole(meta_out, meta_in, meta_s, meta_r).wait_recv()

    for c, (rows, first) in enumerate(CHUNKS):
        lanes = GROUPS * rows
        wins = 2 * rows
        total = SAMP * wins
        spread = jnp.where(iota((GROUPS, lanes), 1) // rows == iota((GROUPS, lanes), 0), 1.0, 0.0)
        slots = lax.dot_general(
            meta_in[...].reshape(GROUPS, 128).astype(F32).astype(BF),
            spread.astype(BF),
            (((0,), (0,)), ((), ())),
            preferred_element_type=F32,
        )
        shape = (total, lanes)
        mine = slots[0:1] == (iota(shape, 0) // wins + 1).astype(F32)
        win = iota(shape, 0) % wins
        lane_r = iota(shape, 1) % rows
        place = [
            jnp.where(mine & (win == h * rows + lane_r), 1.0, 0.0).astype(BF) for h in range(2)
        ]
        whole(snd[c], arr[c], a_s.at[c], a_r.at[c]).wait_recv()
        block = arr[c][...].reshape(lanes, 2 * FH)
        main = jnp.dot(place[0], block[:, :MAIN], preferred_element_type=F32) + jnp.dot(
            place[1], block[:, MAIN : 2 * MAIN], preferred_element_type=F32
        )
        tails = block[:, 2 * MAIN :]
        tail = jnp.where(
            iota((total, 128), 1) < FH - MAIN,
            jnp.dot(place[0], tails, preferred_element_type=F32),
            jnp.dot(place[1], tails, preferred_element_type=F32),
        )
        xf[c][:, pl.ds(0, MAIN)] = main.astype(BF)
        xf[c][:, pl.ds(MAIN, 128)] = tail.astype(BF)
        swap = to_partner(
            xf[c].at[:, pl.ds(0, PAD)], xf[c].at[:, pl.ds(PAD, PAD)], x_s.at[c], x_r.at[c]
        )
        swap.start()
        if c == 0:
            for copy in w_copies:
                copy.wait()
        swap.wait()

        def layer1(n, _, c=c, total=total):
            cols = pl.ds(pl.multiple_of(n * 256, 256), 256)
            pre = jnp.dot(xf[c][...], w1[:, cols], preferred_element_type=F32) + b_first[:, cols]
            hid[pl.ds(0, total), cols] = jax.nn.gelu(pre, approximate=True).astype(BF)
            return 0

        lax.fori_loop(0, HID // 256, layer1, 0)

        def layer2(n, _, c=c, total=total):
            cols = pl.ds(pl.multiple_of(n * 384, 128), 384)
            value = jnp.dot(
                hid[pl.ds(0, total), :], w2[:, cols], preferred_element_type=F32
            )
            ps[c][:, cols] = value.astype(BF)
            return 0

        lax.fori_loop(0, 3, layer2, 0)
        give = to_partner(ps[c], pr[c], p_s.at[c], p_r.at[c])
        give.start()

        def layer2own(n, _, total=total):
            cols = pl.ds(pl.multiple_of(n * 384, 128), 384)
            w_cols = pl.ds(pl.multiple_of(OUT + n * 384, 128), 384)
            value = jnp.dot(
                hid[pl.ds(0, total), :], w2[:, w_cols], preferred_element_type=F32
            )
            po[pl.ds(0, total), cols] = value.astype(BF)
            return 0

        lax.fori_loop(0, 3, layer2own, 0)
        give.wait()
        for n in range(3):
            cols = pl.ds(n * 384, 384)
            summed = po[pl.ds(0, total), cols].astype(F32) + pr[c][:, cols].astype(F32)
            value = (summed + b_second[:, cols]).reshape(SAMP, wins, 384)
            out[:, pl.ds(first, wins), cols] = value.astype(BF)

    whole(meta_out, meta_in, meta_s, meta_r).wait_send()
    for c in range(len(CHUNKS)):
        whole(snd[c], arr[c], a_s.at[c], a_r.at[c]).wait_send()


def shards(encoded, counts, win_ids, dest_seq, dest_slot, w_first, b_first, w_second, b_second):
    smem = pl.BlockSpec(memory_space=pltpu.SMEM)
    vmem = pl.BlockSpec(memory_space=pltpu.VMEM)
    hbm = pl.BlockSpec(memory_space=pl.ANY)
    n = len(CHUNKS)
    sizes = [rows for rows, _ in CHUNKS]
    scratch = [
        pltpu.VMEM((FH, SAMP * CAP), BF),
        pltpu.VMEM((2 * PAD, HID), BF),
        pltpu.VMEM((HID, 2 * OUT), BF),
    ]
    scratch += [pltpu.VMEM((SAMP * r, 2 * FH), BF) for r in sizes]
    scratch += [pltpu.VMEM((GROUPS, r, 2 * FH), BF) for r in sizes] * 2
    scratch += [pltpu.VMEM((GROUPS, 1, 128), I32)] * 2
    scratch += [pltpu.VMEM((SAMP * 2 * r, 2 * PAD), BF) for r in sizes]
    scratch += [pltpu.VMEM((SAMP * 2 * max(sizes), HID), BF)]
    scratch += [pltpu.VMEM((SAMP * 2 * r, OUT), BF) for r in sizes] * 2
    scratch += [pltpu.VMEM((SAMP * 2 * max(sizes), OUT), BF)]
    dma = pltpu.SemaphoreType.DMA
    scratch += [dma, dma((8,)), dma, dma, dma((n,)), dma((n,)), dma((n,)), dma((n,)), dma((n,)), dma((n,))]
    result = pl.pallas_call(
        kernel,
        name="pool_place_project",
        out_shape=jax.ShapeDtypeStruct((SAMP, BLOCK, OUT), BF),
        in_specs=[smem, smem, smem, vmem, vmem, vmem, hbm, hbm, hbm],
        out_specs=vmem,
        scratch_shapes=scratch,
        compiler_params=pltpu.CompilerParams(
            collective_id=0, has_side_effects=True, vmem_limit_bytes=52 << 20
        ),
    )(
        counts, dest_seq, dest_slot, win_ids, b_first.reshape(1, -1), b_second.reshape(1, -1),
        encoded.T, w_first, w_second,
    )
    return result.reshape(SAMP * BLOCK, OUT)


def solution(mesh):
    placed = (
        P("dp", "tensor"),
        P("dp"),
        P("dp", None),
        P("dp"),
        P("dp"),
        P(None, "tensor"),
        P("tensor"),
        P("tensor", None),
        P("tensor"),
    )
    return jax.shard_map(
        shards, mesh=mesh, in_specs=placed, out_specs=P("dp", "tensor"), check_vma=False
    )
```

time: 118 us -> 80.3 us (0.68)
  the two profiles are of different devices: /device:TPU:1 before, /device:TPU:39 now
where the time goes in v1:
time: 80.3 us; the launch traced here: 80 us
  Pallas kernels  72.6 us (90%)
  local copies, waits for them, and re-layouts  7.34 us (9%)
    pallas_call x1, Pallas kernels, shards(): pl.pallas_call(kernel, name='pool_place_project', out_shape=jax.ShapeDtyp...  72.6 us
    unnamed x9, local copies, waits for them, and re-layouts  5.93 us

profile of v1, /device:TPU:39, one launch (start us, length us, event | category | flops | bytes accessed | tf_op | source)
XLA Modules:
  0.0 80.0 jit_solution(8491048438005973983)
XLA Ops:
  0.0 0.7 reshape.10.b_second
  0.7 0.7 reshape.9.b_first
  1.4 0.0 copy-start
  1.4 0.7 copy-done
  2.1 0.0 copy-start.1
  2.1 0.7 copy-done.1
  2.8 0.0 copy-start.2
  2.8 0.7 copy-done.2
  3.4 0.0 copy-start.3
  3.4 0.7 copy-done.3
  4.1 72.6 %pool_place_project.1 = bf16[32,32,1152]{2,1,0:T(8,128)(2,1)} custom-call(s32[32]{0:T(128)S(1)} %copy-done.1, s32[32]{0:T(128)S(1)} %copy-done.2, s32[32]{0:T(128)S(1)} %copy-done.3, s32[32,64]{1,0:T(8,128)S(1)} %copy-done, f32[1,2304]{1,0:T(1,128)S(1)} %reshape.9.b_first, f32[1,1152]{1,0:T(1,128)S(1)} %reshape.10.b_second, bf16[576,2048]{1,0:T(8,128)(2,1)} %bitcast.3, ...), custom_call_target="tpu_custom_call" | custom-call | tf_op jit(solution)/shard_map/pool_place_project/pallas_call | solution.py:306
  76.7 3.3 %copy.11 = bf16[1024,1152]{1,0:T(8,128)(2,1)} copy(bf16[1024,1152]{1,0:T(8,128)(2,1)} %bitcast.2) | data formatting | bytes 4718592
Async XLA Ops:
  1.4 0.7 copy-start
  2.1 0.7 copy-start.1
  2.8 0.7 copy-start.2
  3.4 0.7 copy-start.3

commit v2 on v1

v2 whole, which is shorter than its diff:
```python
import functools

import jax
import jax.numpy as jnp
from jax import lax
from jax.experimental import pallas as pl
from jax.experimental.pallas import tpu as pltpu
from jax.sharding import PartitionSpec as P

MESH = pl.DeviceIdType.MESH
BF = jnp.bfloat16
F32 = jnp.float32
I32 = jnp.int32

GROUPS = 64
SAMP = 32
CAP = 64
BLOCK = 32
FH = 576
MAIN = 512
OUT = 1152
HID = 2304
CHUNKS = ((4, 0), (4, 8), (4, 16), (4, 24))
PAD = 640


def iota(shape, dim):
    return lax.broadcasted_iota(I32, shape, dim)


def div(x, n):
    return lax.shift_right_logical(x, jnp.int32(n.bit_length() - 1))


def mod(x, n):
    return lax.bitwise_and(x, jnp.int32(n - 1))


def peers(me):
    places = []
    for scale in (16, 4, 1):
        here = lax.rem(me // scale, 4)
        places.append([lax.rem(here + d, 4) * scale for d in range(4)])
    for step in range(1, GROUPS):
        off = step * 37 % GROUPS
        yield places[0][off // 16] + places[1][off // 4 % 4] + places[2][off % 4]


def gelu(x):
    half = 0.5 * x
    return half + half * jnp.tanh(x * (0.7978845608028654 + 0.035677408136300125 * (x * x)))


def kernel(*refs):
    n = len(CHUNKS)
    counts_in, seq_in, slot_in, win_in, b_first_in, b_second_in, enc, w_first, w_second, out = refs[:10]
    counts, dest_seq, dest_slot, win_ids, b_first, b_second, tok, w1, w2 = refs[10:19]
    meta_out, meta_in, hid, hot, scale = refs[19:24]
    pooled, snd, arr, xf, ps, pr, po, place, pick = (
        refs[24 + i * n : 24 + (i + 1) * n] for i in range(9)
    )
    in_sem, enc_sem, w_sem, meta_s, meta_r, a_s, a_r, x_s, x_r, p_s, p_r = refs[24 + 9 * n :]
    me = lax.axis_index("dp")
    core = lax.axis_index("tensor")
    other = 1 - core

    barrier = pltpu.get_barrier_semaphore()

    targets = list(peers(me))
    for to in targets:
        pl.semaphore_signal(barrier, inc=1, device_id=(to, core), device_id_type=MESH)
    pl.semaphore_signal(barrier, inc=1, device_id=(me, other), device_id_type=MESH)

    small = [
        pltpu.make_async_copy(src, dst, in_sem.at[i])
        for i, (src, dst) in enumerate(
            (
                (counts_in, counts),
                (seq_in, dest_seq),
                (slot_in, dest_slot),
                (win_in, win_ids),
                (b_first_in, b_first),
                (b_second_in, b_second),
            )
        )
    ]
    for copy in small:
        copy.start()
    enc_copy = pltpu.make_async_copy(enc, tok, enc_sem)
    enc_copy.start()

    w_copies = []
    for side, base in ((0, core * FH), (1, other * FH)):
        at = side * PAD
        w_copies += [(w_first.at[pl.ds(pl.multiple_of(base, 64), MAIN)], w1.at[pl.ds(at, MAIN)])]
        for twice in range(2):
            w_copies += [
                (
                    w_first.at[pl.ds(pl.multiple_of(base + MAIN, 64), 64)],
                    w1.at[pl.ds(at + MAIN + 64 * twice, 64)],
                )
            ]
    w_copies += [
        (w_second.at[:, pl.ds(pl.multiple_of(other * OUT, 128), OUT)], w2.at[:, pl.ds(0, OUT)]),
        (w_second.at[:, pl.ds(pl.multiple_of(core * OUT, 128), OUT)], w2.at[:, pl.ds(OUT, OUT)]),
    ]
    w_copies = [
        pltpu.make_async_copy(src, dst, w_sem.at[i]) for i, (src, dst) in enumerate(w_copies)
    ]

    for copy in small:
        copy.wait()
    row = iota((GROUPS, 128), 0)
    meta = jnp.zeros((GROUPS, 128), I32)
    for s in range(SAMP):
        meta = jnp.where(row == dest_seq[s], dest_slot[s] + 1, meta)
    meta_out[...] = meta.reshape(GROUPS, 1, 128)
    meta_in[pl.ds(me, 1)] = meta_out[pl.ds(me, 1)]

    ids = iota((SAMP, CAP), 1)
    srow = iota((SAMP, CAP), 0)
    limit = jnp.zeros((SAMP, CAP), I32)
    for s in range(SAMP):
        limit = jnp.where(srow == s, counts[s], limit)
    live = jnp.where(ids < limit, win_ids[...], -1)

    rho = iota((128, 256), 0)
    wmap = jnp.zeros((128, 256), I32)
    smap = jnp.zeros((128, 256), I32)
    base = 0
    for rows, first in CHUNKS:
        q = rho - base
        inside = (q >= 0) & (q < 8 * rows)
        h = div(q, 4 * rows)
        wmap = jnp.where(inside, first + h * rows + mod(q, rows), wmap)
        smap = jnp.where(inside, mod(div(q, rows), 4), smap)
        base += 8 * rows
    same = smap == div(iota((128, 256), 1), CAP)

    for g in range(SAMP // 4):
        line = jnp.concatenate([live[4 * g + i : 4 * g + i + 1, :] for i in range(4)], axis=1)
        onehot = jnp.where((wmap == line) & same, 1.0, 0.0).astype(F32)
        number = jnp.sum(onehot, axis=1, keepdims=True)
        hot[g] = onehot.astype(BF)
        scale[g] = jnp.broadcast_to(1.0 / jnp.maximum(number, 1.0), (128, 128))
    for c, (rows, _) in enumerate(CHUNKS):
        lanes = SAMP * rows
        where = jnp.zeros((8, lanes), I32)
        lane_s = div(iota((8, lanes), 1), rows)
        for s in range(SAMP):
            where = jnp.where(lane_s == s, dest_seq[s], where)
        shape = (GROUPS * rows, lanes)
        chosen = (div(iota(shape, 0), rows) == where[0:1]) & (
            mod(iota(shape, 0), rows) == mod(iota(shape, 1), rows)
        )
        pick[c][...] = jnp.where(chosen, 1.0, 0.0).astype(BF)

    enc_copy.wait()
    for copy in w_copies:
        copy.start()

    for g in range(SAMP // 4):
        totals = lax.dot_general(
            hot[g],
            tok[:, pl.ds(256 * g, 256)],
            (((1,), (1,)), ((), ())),
            preferred_element_type=F32,
        )
        mean = totals * scale[g][:, 0:1]
        base = 0
        for c, (rows, _) in enumerate(CHUNKS):
            n = 4 * rows
            lo, hi = mean[base : base + n], mean[base + n : base + 2 * n]
            packed = jnp.concatenate(
                [lo[:, :MAIN], hi[:, :MAIN], lo[:, MAIN:], hi[:, MAIN:]], axis=1
            )
            pooled[c][pl.ds(n * g, n), :] = packed.astype(BF)
            base += 2 * n

    def choose(c):
        rows = CHUNKS[c][0]
        chosen = jnp.dot(pick[c][...], pooled[c][...], preferred_element_type=F32)
        snd[c][...] = chosen.reshape(GROUPS, rows, 2 * FH).astype(BF)
        arr[c][pl.ds(me, 1)] = snd[c][pl.ds(me, 1)]

    def send_all(src, dst, send_sem, recv_sem):
        for to in targets:
            pltpu.make_async_remote_copy(
                src_ref=src.at[pl.ds(to, 1)],
                dst_ref=dst.at[pl.ds(me, 1)],
                send_sem=send_sem,
                recv_sem=recv_sem,
                device_id=(to, core),
                device_id_type=MESH,
            ).start()

    choose(0)
    pl.semaphore_wait(barrier, GROUPS)
    send_all(meta_out, meta_in, meta_s, meta_r)
    send_all(snd[0], arr[0], a_s.at[0], a_r.at[0])
    for c in range(1, len(CHUNKS)):
        choose(c)
        send_all(snd[c], arr[c], a_s.at[c], a_r.at[c])

    def whole(src, dst, send_sem, recv_sem):
        return pltpu.make_async_remote_copy(
            src_ref=src.at[pl.ds(0, GROUPS - 1)],
            dst_ref=dst.at[pl.ds(0, GROUPS - 1)],
            send_sem=send_sem,
            recv_sem=recv_sem,
            device_id=(me, other),
            device_id_type=MESH,
        )

    def to_partner(src, dst, send_sem, recv_sem):
        return pltpu.make_async_remote_copy(
            src_ref=src,
            dst_ref=dst,
            send_sem=send_sem,
            recv_sem=recv_sem,
            device_id=(me, other),
            device_id_type=MESH,
        )

    whole(meta_out, meta_in, meta_s, meta_r).wait_recv()

    for c, (rows, _) in enumerate(CHUNKS):
        lanes = GROUPS * rows
        wins = 2 * rows
        spread = jnp.where(
            div(iota((GROUPS, lanes), 1), rows) == iota((GROUPS, lanes), 0), 1.0, 0.0
        )
        slots = lax.dot_general(
            meta_in[...].reshape(GROUPS, 128).astype(F32).astype(BF),
            spread.astype(BF),
            (((0,), (0,)), ((), ())),
            preferred_element_type=F32,
        )
        shape = (SAMP * wins, lanes)
        mine = slots[0:1] == (div(iota(shape, 0), wins) + 1).astype(F32)
        win = mod(iota(shape, 0), wins)
        lane_r = mod(iota(shape, 1), rows)
        for h in range(2):
            place[c][h] = jnp.where(mine & (win == h * rows + lane_r), 1.0, 0.0).astype(BF)

    def gather(c):
        rows = CHUNKS[c][0]
        lanes = GROUPS * rows
        total = SAMP * 2 * rows
        whole(snd[c], arr[c], a_s.at[c], a_r.at[c]).wait_recv()
        block = arr[c][...].reshape(lanes, 2 * FH)
        main = jnp.dot(place[c][0], block[:, :MAIN], preferred_element_type=F32) + jnp.dot(
            place[c][1], block[:, MAIN : 2 * MAIN], preferred_element_type=F32
        )
        tails = block[:, 2 * MAIN :]
        tail = jnp.where(
            iota((total, 128), 1) < FH - MAIN,
            jnp.dot(place[c][0], tails, preferred_element_type=F32),
            jnp.dot(place[c][1], tails, preferred_element_type=F32),
        )
        xf[c][:, pl.ds(0, MAIN)] = main.astype(BF)
        xf[c][:, pl.ds(MAIN, 128)] = tail.astype(BF)
        swap = to_partner(
            xf[c].at[:, pl.ds(0, PAD)], xf[c].at[:, pl.ds(PAD, PAD)], x_s.at[c], x_r.at[c]
        )
        swap.start()
        return swap

    def layer1(c):
        total = SAMP * 2 * CHUNKS[c][0]
        for n in range(HID // 256):
            cols = pl.ds(n * 256, 256)
            pre = jnp.dot(xf[c][...], w1[:, cols], preferred_element_type=F32)
            pre = pre + b_first[cols].reshape(1, 256)
            hid[pl.ds(0, total), cols] = gelu(pre).astype(BF)

    def layer2(c, tiles):
        total = SAMP * 2 * CHUNKS[c][0]
        for n in tiles:
            cols = pl.ds(n * 256, 256)
            value = jnp.dot(hid[pl.ds(0, total), :], w2[:, cols], preferred_element_type=F32)
            value = value.astype(BF)
            if n < 4:
                ps[c][:, cols] = value
            elif n == 4:
                ps[c][:, pl.ds(1024, 128)] = value[:, :128]
                po[c][:, pl.ds(0, 128)] = value[:, 128:]
            else:
                po[c][:, pl.ds(n * 256 - OUT, 256)] = value

    def finish(c):
        rows, first = CHUNKS[c]
        for n in range(3):
            cols = pl.ds(n * 384, 384)
            summed = po[c][:, cols].astype(F32) + pr[c][:, cols].astype(F32)
            value = (summed + b_second[cols].reshape(1, 384)).reshape(SAMP, 2 * rows, 384)
            out[:, pl.ds(first, 2 * rows), cols] = value.astype(BF)

    swap = gather(0)
    for copy in w_copies:
        copy.wait()
    pending = None
    for c in range(len(CHUNKS)):
        last = c == len(CHUNKS) - 1
        if pending is not None:
            pending.wait()
            finish(c - 1)
        swap.wait()
        layer1(c)
        layer2(c, range(5))
        give = to_partner(ps[c], pr[c], p_s.at[c], p_r.at[c])
        give.start()
        if not last:
            swap = gather(c + 1)
        layer2(c, range(5, 9))
        pending = give
    pending.wait()
    finish(len(CHUNKS) - 1)

    whole(meta_out, meta_in, meta_s, meta_r).wait_send()
    for c in range(len(CHUNKS)):
        whole(snd[c], arr[c], a_s.at[c], a_r.at[c]).wait_send()


def shards(encoded, counts, win_ids, dest_seq, dest_slot, w_first, b_first, w_second, b_second):
    vmem = pl.BlockSpec(memory_space=pltpu.VMEM)
    hbm = pl.BlockSpec(memory_space=pltpu.HBM)
    n = len(CHUNKS)
    sizes = [rows for rows, _ in CHUNKS]
    scratch = [pltpu.SMEM((SAMP,), I32)] * 3
    scratch += [
        pltpu.VMEM((SAMP, CAP), I32),
        pltpu.VMEM((HID,), F32),
        pltpu.VMEM((OUT,), F32),
        pltpu.VMEM((FH, SAMP * CAP), BF),
        pltpu.VMEM((2 * PAD, HID), BF),
        pltpu.VMEM((HID, 2 * OUT), BF),
    ]
    scratch += [pltpu.VMEM((GROUPS, 1, 128), I32)] * 2
    scratch += [pltpu.VMEM((SAMP * 2 * max(sizes), HID), BF)]
    scratch += [pltpu.VMEM((SAMP // 4, 128, 256), BF), pltpu.VMEM((SAMP // 4, 128, 128), F32)]
    scratch += [pltpu.VMEM((SAMP * r, 2 * FH), BF) for r in sizes]
    scratch += [pltpu.VMEM((GROUPS, r, 2 * FH), BF) for r in sizes] * 2
    scratch += [pltpu.VMEM((SAMP * 2 * r, 2 * PAD), BF) for r in sizes]
    scratch += [pltpu.VMEM((SAMP * 2 * r, OUT), BF) for r in sizes] * 3
    scratch += [pltpu.VMEM((2, SAMP * 2 * r, GROUPS * r), BF) for r in sizes]
    scratch += [pltpu.VMEM((GROUPS * r, SAMP * r), BF) for r in sizes]
    dma = pltpu.SemaphoreType.DMA
    scratch += [dma((6,)), dma, dma((8,)), dma, dma, dma((n,)), dma((n,)), dma((n,)), dma((n,)), dma((n,)), dma((n,))]
    result = pl.pallas_call(
        kernel,
        name="pool_place_project",
        out_shape=pltpu.VMEM((SAMP, BLOCK, OUT), BF),
        in_specs=[hbm] * 9,
        out_specs=vmem,
        scratch_shapes=scratch,
        compiler_params=pltpu.CompilerParams(
            collective_id=0, has_side_effects=True, vmem_limit_bytes=52 << 20
        ),
    )(
        counts, dest_seq, dest_slot, win_ids, b_first, b_second,
        encoded.T, w_first, w_second,
    )
    return result.reshape(SAMP * BLOCK, OUT)


def solution(mesh):
    placed = (
        P("dp", "tensor"),
        P("dp"),
        P("dp", None),
        P("dp"),
        P("dp"),
        P(None, "tensor"),
        P("tensor"),
        P("tensor", None),
        P("tensor"),
    )
    return jax.shard_map(
        shards, mesh=mesh, in_specs=placed, out_specs=P("dp", "tensor"), check_vma=False
    )
```

time: 80.3 us -> 49.1 us (0.61)
  the two profiles are of different devices: /device:TPU:39 before, /device:TPU:1 now
where the time goes in v2:
time: 49.1 us; the launch traced here: 48.9 us
  Pallas kernels  47.5 us (97%)
  local copies, waits for them, and re-layouts  1.41 us (3%)
    pallas_call x1, Pallas kernels, shards(): pl.pallas_call(kernel, name='pool_place_project', out_shape=pltpu.VMEM((S...  47.5 us
    unnamed x1, local copies, waits for them, and re-layouts  1.41 us

profile of v2, /device:TPU:1, one launch (start us, length us, event | category | flops | bytes accessed | tf_op | source)
XLA Modules:
  0.0 48.9 jit_solution(18104869728345305760)
XLA Ops:
  0.0 47.5 %pool_place_project.1 = bf16[32,32,1152]{2,1,0:T(8,128)(2,1)S(1)} custom-call(s32[32]{0:T(128)} %refs_0_.1, s32[32]{0:T(128)} %refs_1_.1, s32[32]{0:T(128)} %refs_2_.1, s32[32,64]{1,0:T(8,128)} %refs_3_.1, f32[2304]{0:T(1024)} %refs_4_.1, f32[1152]{0:T(1024)} %refs_5_.1, bf16[576,2048]{1,0:T(8,128)(2,1)} %bitcast.3, bf16[1152,2304]{1,0:T(8,128)(2,1)} %refs_7_.1, ...), custom_call_target="tpu_custom_call" | custom-call | tf_op jit(solution)/shard_map/pool_place_project/pallas_call | solution.py:350
  47.5 1.4 %copy.11 = bf16[1024,1152]{1,0:T(8,128)(2,1)} copy(bf16[1024,1152]{1,0:T(8,128)(2,1)S(1)} %bitcast.2) | data formatting | bytes 4718592

commit v3 on v2

--- a/solution.py
+++ b/solution.py
@@ -20,7 +20,8 @@
 MAIN = 512
 OUT = 1152
 HID = 2304
-CHUNKS = ((4, 0), (4, 8), (4, 16), (4, 24))
+CHUNKS = tuple((2, 4 * c) for c in range(8))
+EARLY = 8
 PAD = 640
 
 
@@ -34,6 +35,10 @@
 
 def mod(x, n):
     return lax.bitwise_and(x, jnp.int32(n - 1))
+
+
+def hops(off):
+    return sum(min(d, 4 - d) for d in off)
 
 
 def peers(me):
@@ -41,9 +46,13 @@
     for scale in (16, 4, 1):
         here = lax.rem(me // scale, 4)
         places.append([lax.rem(here + d, 4) * scale for d in range(4)])
-    for step in range(1, GROUPS):
-        off = step * 37 % GROUPS
-        yield places[0][off // 16] + places[1][off // 4 % 4] + places[2][off % 4]
+    offsets = [(i // 16, i // 4 % 4, i % 4) for i in range(1, GROUPS)]
+    done = []
+    for off in sorted(offsets, key=lambda o: -hops(o)):
+        for one in (off, tuple((4 - d) % 4 for d in off)):
+            if one not in done:
+                done.append(one)
+    return [sum(places[i][d] for i, d in enumerate(off)) for off in done]
 
 
 def gelu(x):
@@ -66,7 +75,7 @@
 
     barrier = pltpu.get_barrier_semaphore()
 
-    targets = list(peers(me))
+    targets = peers(me)
     for to in targets:
         pl.semaphore_signal(barrier, inc=1, device_id=(to, core), device_id_type=MESH)
     pl.semaphore_signal(barrier, inc=1, device_id=(me, other), device_id_type=MESH)
@@ -198,7 +207,7 @@
     pl.semaphore_wait(barrier, GROUPS)
     send_all(meta_out, meta_in, meta_s, meta_r)
     send_all(snd[0], arr[0], a_s.at[0], a_r.at[0])
-    for c in range(1, len(CHUNKS)):
+    for c in range(1, EARLY):
         choose(c)
         send_all(snd[c], arr[c], a_s.at[c], a_r.at[c])
 
@@ -241,25 +250,27 @@
         win = mod(iota(shape, 0), wins)
         lane_r = mod(iota(shape, 1), rows)
         for h in range(2):
-            place[c][h] = jnp.where(mine & (win == h * rows + lane_r), 1.0, 0.0).astype(BF)
+            mask = jnp.where(mine & (win == h * rows + lane_r), 1.0, 0.0)
+            place[c][:, pl.ds(h * lanes, lanes)] = mask.astype(BF)
 
     def gather(c):
         rows = CHUNKS[c][0]
         lanes = GROUPS * rows
-        total = SAMP * 2 * rows
         whole(snd[c], arr[c], a_s.at[c], a_r.at[c]).wait_recv()
         block = arr[c][...].reshape(lanes, 2 * FH)
-        main = jnp.dot(place[c][0], block[:, :MAIN], preferred_element_type=F32) + jnp.dot(
-            place[c][1], block[:, MAIN : 2 * MAIN], preferred_element_type=F32
-        )
-        tails = block[:, 2 * MAIN :]
-        tail = jnp.where(
-            iota((total, 128), 1) < FH - MAIN,
-            jnp.dot(place[c][0], tails, preferred_element_type=F32),
-            jnp.dot(place[c][1], tails, preferred_element_type=F32),
-        )
-        xf[c][:, pl.ds(0, MAIN)] = main.astype(BF)
-        xf[c][:, pl.ds(MAIN, 128)] = tail.astype(BF)
+        tails = block[:, 2 * MAIN :].astype(F32)
+        low = iota((lanes, 128), 1) < FH - MAIN
+        zero = jnp.zeros_like(tails)
+        halves = [
+            jnp.concatenate(
+                [block[:, h * MAIN : (h + 1) * MAIN], jnp.where(low, *pair).astype(BF)], axis=1
+            )
+            for h, pair in enumerate(((tails, zero), (zero, tails)))
+        ]
+        placed = jnp.dot(
+            place[c][...], jnp.concatenate(halves, axis=0), preferred_element_type=F32
+        )
+        xf[c][:, pl.ds(0, PAD)] = placed.astype(BF)
         swap = to_partner(
             xf[c].at[:, pl.ds(0, PAD)], xf[c].at[:, pl.ds(PAD, PAD)], x_s.at[c], x_r.at[c]
         )
@@ -297,22 +308,29 @@
             out[:, pl.ds(first, 2 * rows), cols] = value.astype(BF)
 
     swap = gather(0)
+    for c in range(EARLY, len(CHUNKS)):
+        choose(c)
+        send_all(snd[c], arr[c], a_s.at[c], a_r.at[c])
     for copy in w_copies:
         copy.wait()
     pending = None
     for c in range(len(CHUNKS)):
         last = c == len(CHUNKS) - 1
+        swap.wait()
+        layer1(c)
+        if not last:
+            swap = gather(c + 1)
         if pending is not None:
             pending.wait()
+        give = to_partner(ps[c], pr[c], p_s.at[c], p_r.at[c])
+        layer2(c, range(5))
+        if last:
+            give.start()
+        if pending is not None:
             finish(c - 1)
-        swap.wait()
-        layer1(c)
-        layer2(c, range(5))
-        give = to_partner(ps[c], pr[c], p_s.at[c], p_r.at[c])
-        give.start()
+        layer2(c, range(5, 9))
         if not last:
-            swap = gather(c + 1)
-        layer2(c, range(5, 9))
+            give.start()
         pending = give
     pending.wait()
     finish(len(CHUNKS) - 1)
@@ -343,7 +361,7 @@
     scratch += [pltpu.VMEM((GROUPS, r, 2 * FH), BF) for r in sizes] * 2
     scratch += [pltpu.VMEM((SAMP * 2 * r, 2 * PAD), BF) for r in sizes]
     scratch += [pltpu.VMEM((SAMP * 2 * r, OUT), BF) for r in sizes] * 3
-    scratch += [pltpu.VMEM((2, SAMP * 2 * r, GROUPS * r), BF) for r in sizes]
+    scratch += [pltpu.VMEM((SAMP * 2 * r, 2 * GROUPS * r), BF) for r in sizes]
     scratch += [pltpu.VMEM((GROUPS * r, SAMP * r), BF) for r in sizes]
     dma = pltpu.SemaphoreType.DMA
     scratch += [dma((6,)), dma, dma((8,)), dma, dma, dma((n,)), dma((n,)), dma((n,)), dma((n,)), dma((n,)), dma((n,))]

time: 49.1 us -> 49 us (level)
  no operation moved by 1% of the time
where the time goes in v3:
time: 49 us; the launch traced here: 48.8 us
  Pallas kernels  47.4 us (97%)
  local copies, waits for them, and re-layouts  1.41 us (3%)
    pallas_call x1, Pallas kernels, shards(): pl.pallas_call(kernel, name='pool_place_project', out_shape=pltpu.VMEM((S...  47.4 us
    unnamed x1, local copies, waits for them, and re-layouts  1.41 us

profile of v3, /device:TPU:1, one launch (start us, length us, event | category | flops | bytes accessed | tf_op | source)
XLA Modules:
  0.0 48.8 jit_solution(3330033490098575159)
XLA Ops:
  0.0 47.4 %pool_place_project.1 = bf16[32,32,1152]{2,1,0:T(8,128)(2,1)S(1)} custom-call(s32[32]{0:T(128)} %refs_0_.1, s32[32]{0:T(128)} %refs_1_.1, s32[32]{0:T(128)} %refs_2_.1, s32[32,64]{1,0:T(8,128)} %refs_3_.1, f32[2304]{0:T(1024)} %refs_4_.1, f32[1152]{0:T(1024)} %refs_5_.1, bf16[576,2048]{1,0:T(8,128)(2,1)} %bitcast.3, bf16[1152,2304]{1,0:T(8,128)(2,1)} %refs_7_.1, ...), custom_call_target="tpu_custom_call" | custom-call | tf_op jit(solution)/shard_map/pool_place_project/pallas_call | solution.py:368
  47.4 1.4 %copy.11 = bf16[1024,1152]{1,0:T(8,128)(2,1)} copy(bf16[1024,1152]{1,0:T(8,128)(2,1)S(1)} %bitcast.2) | data formatting | bytes 4718592

commit v4 on v3

--- a/solution.py
+++ b/solution.py
@@ -21,7 +21,7 @@
 OUT = 1152
 HID = 2304
 CHUNKS = tuple((2, 4 * c) for c in range(8))
-EARLY = 8
+LAG = 2
 PAD = 640
 
 
@@ -109,10 +109,11 @@
                     w1.at[pl.ds(at + MAIN + 64 * twice, 64)],
                 )
             ]
-    w_copies += [
-        (w_second.at[:, pl.ds(pl.multiple_of(other * OUT, 128), OUT)], w2.at[:, pl.ds(0, OUT)]),
-        (w_second.at[:, pl.ds(pl.multiple_of(core * OUT, 128), OUT)], w2.at[:, pl.ds(OUT, OUT)]),
-    ]
+    for at, base in ((0, other * OUT), (OUT, core * OUT)):
+        for half in range(2):
+            rows = pl.ds(half * (HID // 2), HID // 2)
+            columns = pl.ds(pl.multiple_of(base, 128), OUT)
+            w_copies.append((w_second.at[rows, columns], w2.at[rows, pl.ds(at, OUT)]))
     w_copies = [
         pltpu.make_async_copy(src, dst, w_sem.at[i]) for i, (src, dst) in enumerate(w_copies)
     ]
@@ -165,8 +166,6 @@
         pick[c][...] = jnp.where(chosen, 1.0, 0.0).astype(BF)
 
     enc_copy.wait()
-    for copy in w_copies:
-        copy.start()
 
     for g in range(SAMP // 4):
         totals = lax.dot_general(
@@ -207,9 +206,15 @@
     pl.semaphore_wait(barrier, GROUPS)
     send_all(meta_out, meta_in, meta_s, meta_r)
     send_all(snd[0], arr[0], a_s.at[0], a_r.at[0])
-    for c in range(1, EARLY):
-        choose(c)
-        send_all(snd[c], arr[c], a_s.at[c], a_r.at[c])
+    parts = [w_copies[0:3], w_copies[3:6]] + [w_copies[i : i + 1] for i in range(6, 10)]
+    for c in range(1, len(CHUNKS) + LAG):
+        if c < len(CHUNKS):
+            choose(c)
+        if c > LAG:
+            send_all(snd[c - LAG], arr[c - LAG], a_s.at[c - LAG], a_r.at[c - LAG])
+        if 0 <= c - 2 < len(parts):
+            for copy in parts[c - 2]:
+                copy.start()
 
     def whole(src, dst, send_sem, recv_sem):
         return pltpu.make_async_remote_copy(
@@ -308,9 +313,6 @@
             out[:, pl.ds(first, 2 * rows), cols] = value.astype(BF)
 
     swap = gather(0)
-    for c in range(EARLY, len(CHUNKS)):
-        choose(c)
-        send_all(snd[c], arr[c], a_s.at[c], a_r.at[c])
     for copy in w_copies:
         copy.wait()
     pending = None
@@ -364,7 +366,7 @@
     scratch += [pltpu.VMEM((SAMP * 2 * r, 2 * GROUPS * r), BF) for r in sizes]
     scratch += [pltpu.VMEM((GROUPS * r, SAMP * r), BF) for r in sizes]
     dma = pltpu.SemaphoreType.DMA
-    scratch += [dma((6,)), dma, dma((8,)), dma, dma, dma((n,)), dma((n,)), dma((n,)), dma((n,)), dma((n,)), dma((n,))]
+    scratch += [dma((6,)), dma, dma((10,)), dma, dma, dma((n,)), dma((n,)), dma((n,)), dma((n,)), dma((n,)), dma((n,))]
     result = pl.pallas_call(
         kernel,
         name="pool_place_project",

time: 49 us -> 48.4 us (0.988)
  Pallas kernels: 47.4 us -> 46.8 us
    pallas_call x1, Pallas kernels: 47.4 us -> 46.8 us  [shards(): pl.pallas_call(kernel, name='pool_place_project', out_shape=pltpu.VMEM((S...]
where the time goes in v4:
time: 48.4 us; the launch traced here: 48.2 us
  Pallas kernels  46.8 us (97%)
  local copies, waits for them, and re-layouts  1.41 us (3%)
    pallas_call x1, Pallas kernels, shards(): pl.pallas_call(kernel, name='pool_place_project', out_shape=pltpu.VMEM((S...  46.8 us
    unnamed x1, local copies, waits for them, and re-layouts  1.41 us

profile of v4, /device:TPU:1, one launch (start us, length us, event | category | flops | bytes accessed | tf_op | source)
XLA Modules:
  0.0 48.2 jit_solution(12579805356750270661)
XLA Ops:
  0.0 46.8 %pool_place_project.1 = bf16[32,32,1152]{2,1,0:T(8,128)(2,1)S(1)} custom-call(s32[32]{0:T(128)} %refs_0_.1, s32[32]{0:T(128)} %refs_1_.1, s32[32]{0:T(128)} %refs_2_.1, s32[32,64]{1,0:T(8,128)} %refs_3_.1, f32[2304]{0:T(1024)} %refs_4_.1, f32[1152]{0:T(1024)} %refs_5_.1, bf16[576,2048]{1,0:T(8,128)(2,1)} %bitcast.3, bf16[1152,2304]{1,0:T(8,128)(2,1)} %refs_7_.1, ...), custom_call_target="tpu_custom_call" | custom-call | tf_op jit(solution)/shard_map/pool_place_project/pallas_call | solution.py:370
  46.8 1.4 %copy.11 = bf16[1024,1152]{1,0:T(8,128)(2,1)} copy(bf16[1024,1152]{1,0:T(8,128)(2,1)S(1)} %bitcast.2) | data formatting | bytes 4718592
